TPU v7x, 32 devices: a whole 2x2x4 slice. The times are simulated.
32 devices in a mesh: section: 4 (over y, core), seq: 8 (over z, x).
Axes of the slice: x: 2, y: 2, z: 4, core: 2. Of those that a mesh axis runs over, the one named last changes fastest.
Arguments:
- acts: bfloat16 [4, 1024, 2560], P('section', 'seq'), may hold values from -6 to 6
- feed: bfloat16 [1, 1024, 2560], P(None, 'seq'), may hold values from -6 to 6
- norm_gain: float32 [4, 2560], P('section'), may hold values from 0.5 to 1.5
- conv_weight: bfloat16 [4, 4, 2560], P('section'), may hold values from -3 to 3
- conv_bias: float32 [4, 2560], P('section'), may hold values from -3 to 3
- x_proj: bfloat16 [4, 2560, 192], P('section'), may hold values from -0.125 to 0.125
- dt_proj: bfloat16 [4, 160, 2560], P('section'), may hold values from -0.5 to 0.5
- dt_bias: float32 [4, 2560], P('section'), may hold values from -3 to 0.5
- a_rate: float32 [4, 16, 2560], P('section'), may hold values from 1.953125e-05 to 0.5
- skip: float32 [4, 2560], P('section'), may hold values from 0.5 to 1.5
Outputs:
- layer_outputs: bfloat16 [2, 4, 1024, 2560], P(None, 'section', 'seq')
All inputs are finite; a program needn't handle non-finite values.
Results may differ from a plain program's by a relative error of at most 0.0062.
Values may be sent and summed in bfloat16 or wider, within the bound.
A program may use at most 64 MiB of HBM per device.

v0:
```python
import math

import jax
import jax.numpy as jnp
from jax import lax
from jax.sharding import PartitionSpec as P

STATE = 16
RANK = 160
KERNEL = 4
TICKS = 2


def prefix(shard, axis, combine, identity):
    size, position = (lax.axis_size(axis), lax.axis_index(axis))
    everything = jax.tree.map(lambda part: lax.all_gather(part, axis), shard)
    start = jax.tree.map(
        lambda part, zero: jnp.broadcast_to(jnp.asarray(zero, part.dtype), part.shape),
        shard,
        identity,
    )

    def step(k, before):
        reached = k < position
        new = combine(before, jax.tree.map(lambda part: part[k], everything))
        return jax.tree.map(lambda a, b: jnp.where(reached, a, b), new, before)

    return lax.fori_loop(0, size, step, start)


def passed_along(value, axis, steps):
    count = lax.axis_size(axis)
    initial, last = (max(0, -steps), min(count, count - steps))
    return lax.ppermute(value, axis, [(source, source + steps) for source in range(initial, last)])


def rms_rows(rows, gain):
    values = rows.astype(jnp.float32)
    return values * lax.rsqrt(jnp.mean(values * values, axis=-1, keepdims=True) + 1e-05) * gain


def pass_carries(totals, ends, rates):

    def link(earlier, later):
        return (earlier[0] + later[0], jnp.exp(-rates * later[0][None, :]) * earlier[1] + later[1])

    empty = (jnp.zeros_like(totals), jnp.zeros_like(ends))
    _, incoming = prefix((totals, ends), "seq", link, empty)
    return incoming


def token_scan(start, steps, drive, bmat, cmat, rates):
    rows = steps.shape[0]
    width = steps.shape[1]
    blocks = math.gcd(rows, 16)
    group = rows // blocks
    packed = (
        steps.reshape(blocks, group, width),
        drive.reshape(blocks, group, width),
        bmat.reshape(blocks, group, STATE),
        cmat.reshape(blocks, group, STATE),
    )

    def advance(state, piece):
        step_blk, drive_blk, b_blk, c_blk = piece
        emitted = []
        for inner_t in range(group):
            state = (
                jnp.exp(-step_blk[inner_t][None, :] * rates) * state
                + b_blk[inner_t][:, None] * drive_blk[inner_t][None, :]
            )
            emitted.append(jnp.sum(c_blk[inner_t][:, None] * state, axis=0))
        return (state, jnp.stack(emitted, 0))

    final, outputs = lax.scan(advance, start, packed)
    return (final, outputs.reshape(rows, width))


def layer(current, before, gain, conv_w, conv_b, x_w, dt_w, dt_b, rates, skip_w):
    rows = current.shape[0]
    width = current.shape[1]
    joined = rms_rows(jnp.concatenate([before, current], 0), gain)
    conv = jnp.zeros((rows, width), jnp.float32) + conv_b
    for shift_k in range(KERNEL):
        conv = conv + conv_w[shift_k].astype(jnp.float32) * joined[shift_k : shift_k + rows]
    mixed = jax.nn.silu(conv).astype(jnp.bfloat16)
    proj = jnp.dot(mixed, x_w, preferred_element_type=jnp.float32)
    dt_low = proj[:, :RANK].astype(jnp.bfloat16)
    bmat = proj[:, RANK : RANK + STATE]
    cmat = proj[:, RANK + STATE :]
    steps = jax.nn.softplus(jnp.dot(dt_low, dt_w, preferred_element_type=jnp.float32) + dt_b)
    inputs = mixed.astype(jnp.float32)
    drive = steps * inputs
    summed = jnp.cumsum(steps, axis=0)
    zero_state = jnp.zeros((STATE, width), jnp.float32)
    ends, local_out = token_scan(zero_state, steps, drive, bmat, cmat, rates)
    incoming = pass_carries(summed[-1], ends, rates)
    fixed = jnp.zeros((rows, width), jnp.float32)
    for state_n in range(STATE):
        fixed = (
            fixed
            + cmat[:, state_n : state_n + 1]
            * jnp.exp(-summed * rates[state_n][None, :])
            * incoming[state_n][None, :]
        )
    outputs = local_out + fixed
    return (outputs + skip_w * inputs).astype(jnp.bfloat16)


def local(acts, feed, norm_gain, conv_weight, conv_bias, x_proj, dt_proj, dt_bias, a_rate, skip):
    margin = KERNEL - 1
    section_zero = lax.axis_index("section") == 0
    seq_zero = lax.axis_index("seq") == 0
    weights = (
        norm_gain[0],
        conv_weight[0],
        conv_bias[0],
        x_proj[0],
        dt_proj[0],
        dt_bias[0],
        a_rate[0],
        skip[0],
    )
    current = acts[0]
    prev_now, prev_feeds = passed_along((acts[0][-margin:], feed[:, -margin:, :]), "seq", 1)
    results = []
    for tick in range(TICKS):
        result = layer(current, prev_now, *weights)
        results.append(result)
        if tick + 1 < TICKS:
            received = passed_along(result, "section", 1)
            current = jnp.where(section_zero, feed[tick], received)
            diagonal = passed_along(result[-margin:], ("section", "seq"), lax.axis_size("seq") + 1)
            diagonal = jnp.where(seq_zero, jnp.zeros_like(diagonal), diagonal)
            prev_now = jnp.where(section_zero, prev_feeds[tick], diagonal)
    return jnp.stack(results, 0)[:, None]


def solution(mesh):
    return jax.shard_map(
        local,
        mesh=mesh,
        in_specs=(
            P("section", "seq", None),
            P(None, "seq", None),
            P("section", None),
            P("section", None, None),
            P("section", None),
            P("section", None, None),
            P("section", None, None),
            P("section", None),
            P("section", None, None),
            P("section", None),
        ),
        out_specs=P(None, "section", "seq", None),
        check_vma=False,
    )
```

profile of v0, /device:TPU:0, one launch (start us, length us, event | category | flops | bytes accessed | tf_op | source)
XLA Modules:
  0.0 301.0 jit_solution(11971880597575109144)
XLA Ops:
  7.5 4.9 %collective-permute-start = (bf16[3,2560]{1,0:T(4,128)(2,1)S(1)}, bf16[3,2560]{1,0:T(4,128)(2,1)S(1)}, u32[]{:S(2)}, u32[]{:S(2)}) collective-permute-start(bf16[3,2560]{1,0:T(4,128)(2,1)S(1)} %slice_bitcast_fusion.32), channel_id=1, source_target_pairs={{0,1},{1,2},{2,3},{3,4},{4,5},{5,6},{6,7},{8,9},{9,10},{10,11},{11... | collective-permute-start | bytes 46088 | tf_op jit(solution)/shard_map/ppermute | solution.py:34
  22.8 65.1 %while.58 = (s32[]{:T(128)}, f32[16,2560]{1,0:T(8,128)S(1)}, f32[16,8,2560]{2,1,0:T(8,128)}, f32[16,8,2560]{2,1,0:T(8,128)}, f32[16,2560]{1,0:T(8,128)S(1)}, /*i...) while((s32[]{:T(128)}, f32[16,2560]{1,0:T(8,128)S(1)}, ...), condition=%wide.region_10.11_spmd.clone, body=%wide.region_1.10_spmd.clone.sunk | while | flops 2867210 | bytes 3139680 | solution.py:75
  26.6 2.3 dynamic-slice_reduce_fusion.22
  38.6 2.3 dynamic-slice_reduce_fusion.22
  42.7 2.3 dynamic-slice_reduce_fusion.22
  63.1 2.3 dynamic-slice_reduce_fusion.22
  67.2 2.3 dynamic-slice_reduce_fusion.22
  71.4 2.6 dynamic-slice_reduce_fusion.22
  75.8 2.3 dynamic-slice_reduce_fusion.22
  83.8 2.3 dynamic-slice_reduce_fusion.22
  90.0 4.0 %collective-permute-start.1 = (bf16[1,3,2560]{2,1,0:T(4,128)(2,1)}, bf16[1,3,2560]{2,1,0:T(4,128)(2,1)}, u32[]{:S(2)}, u32[]{:S(2)}) collective-permute-start(bf16[1,3,2560]{2,1,0:T(4,128)(2,1)} %slice.704), channel_id=1, source_target_pairs={{0,1},{1,2},{2,3},{3,4},{4,5},{5,6},{6,7},{8,9},{9,10},{10,11},{11... | collective-permute-start | bytes 46088 | tf_op jit(solution)/shard_map/ppermute | solution.py:34
  95.7 3.5 %reduce_window_sum.17 = f32[128,2560]{1,0:T(8,128)} reduce-window(f32[128,2560]{1,0:T(8,128)} %bitcast.220, f32[]{:T(128)} %constant.113.clone.1), window={size=128x1 pad=127_0x0_0}, to_apply=%region_11.12 | reduce-window | flops 41615360 | bytes 2621444 | tf_op jit(solution)/shard_map/jit(cumsum)/reduce_window_sum | solution.py:94
  100.1 30.9 %all-gather.2 = f32[8,1,2560]{2,1,0:T(1,128)S(1)} all-gather(f32[1,1,2560]{2,1,0:T(1,128)S(1)} %slice_bitcast_fusion.34), channel_id=1, replica_groups=mesh['section'=4,'seq'=8] {'seq'}, dimensions={0}, use_global_device_ids=true | all-gather | bytes 92160 | tf_op jit(solution)/shard_map/all_gather | solution.py:16
  131.7 8.7 %while.59 = (s32[]{:T(128)}, f32[16,2560]{1,0:T(8,128)S(1)}, s32[]{:T(128)}, f32[8,2560]{1,0:T(8,128)S(1)}, f32[16,2560]{1,0:T(8,128)S(1)}, /*index=5*/f32[8,16,2560]{2,1,0:T(8,128)}, s32[]{:T(128)}, s32[]{:T(128)}) while((s32[]{:T(128)}, f32[16,2560]{1,0:T(8,128)S(1)}, s32[]{:T(128)}, f32[8,2560]{1,0:T(8,128)S(1)}, ...), condition=%wide.region_13.14_spmd.clone, body=%wide.region_12.13_spmd.clone.sunk | while | flops 204804 | bytes 686193 | solution.py:28
  140.9 7.2 %fusion.26 = bf16[128,2560]{1,0:T(8,128)(2,1)S(1)} fusion(f32[16,8,2560]{2,1,0:T(8,128)} %get-tuple-element.389, f32[128,2560]{1,0:T(8,128)} %reduce_window_sum.17, f32[2560]{0:T(1024)} %reduce.73, f32[2560]{0:T(1024)S(1)} %get-tuple-element.599, f32[2560]{0:T(1024)} %get-tuple-element.583, f32[128]{0:T(128)S(1)} %get-tuple-element.740, ...), kind=kLoop, calls=%fused_computation.144 | loop fusion | flops 26869760 | bytes 8916992 | tf_op jit(solution)/shard_map/convert_element_type | solution.py:107
  149.5 3.9 %collective-permute-start.3 = (bf16[128,2560]{1,0:T(8,128)(2,1)S(1)}, bf16[128,2560]{1,0:T(8,128)(2,1)S(1)}, u32[]{:S(2)}, u32[]{:S(2)}) collective-permute-start(bf16[128,2560]{1,0:T(8,128)(2,1)S(1)} %fusion.26), channel_id=1, source_target_pairs={{0,8},{8,16},{16,24},{1,9},{9,17},{17,25},{2,10},{10,18},{18,26},{... | collective-permute-start | bytes 1966088 | tf_op jit(solution)/shard_map/ppermute | solution.py:34
  162.1 65.1 %while.60 = (s32[]{:T(128)}, f32[16,2560]{1,0:T(8,128)S(1)}, f32[16,8,2560]{2,1,0:T(8,128)}, f32[16,8,2560]{2,1,0:T(8,128)}, f32[16,2560]{1,0:T(8,128)S(1)}, /*i...) while((s32[]{:T(128)}, f32[16,2560]{1,0:T(8,128)S(1)}, ...), condition=%wide.region_24.25_spmd.clone, body=%wide.region_15.24_spmd.clone.sunk | while | flops 2867210 | bytes 3139680 | solution.py:75
  165.9 2.3 dynamic-slice_reduce_fusion.24
  178.0 2.3 dynamic-slice_reduce_fusion.24
  182.1 2.3 dynamic-slice_reduce_fusion.24
  194.3 2.3 dynamic-slice_reduce_fusion.24
  198.4 2.3 dynamic-slice_reduce_fusion.24
  202.5 2.3 dynamic-slice_reduce_fusion.24
  206.6 2.3 dynamic-slice_reduce_fusion.24
  210.8 2.6 dynamic-slice_reduce_fusion.24
  215.2 2.3 dynamic-slice_reduce_fusion.24
  223.1 2.3 dynamic-slice_reduce_fusion.24
  228.0 3.5 %reduce_window_sum.18 = f32[128,2560]{1,0:T(8,128)} reduce-window(f32[128,2560]{1,0:T(8,128)} %bitcast.222, f32[]{:T(128)} %constant.113.clone.1), window={size=128x1 pad=127_0x0_0}, to_apply=%region_25.26 | reduce-window | flops 41615360 | bytes 2621444 | tf_op jit(solution)/shard_map/jit(cumsum)/reduce_window_sum | solution.py:94
  232.3 30.7 %all-gather.3 = f32[8,1,2560]{2,1,0:T(1,128)S(1)} all-gather(f32[1,1,2560]{2,1,0:T(1,128)S(1)} %slice_bitcast_fusion.33), channel_id=1, replica_groups=mesh['section'=4,'seq'=8] {'seq'}, dimensions={0}, use_global_device_ids=true | all-gather | bytes 92160 | tf_op jit(solution)/shard_map/all_gather | solution.py:16
  263.0 13.3 %all-gather.9.cloned.1.call-done = f32[128,2560]{1,0:T(8,128)} async-done(((f32[16,2560]{1,0:T(8,128)}), f32[128,2560]{1,0:T(8,128)}) %all-gather.9.cloned.1.call-update) | async-done | bytes 1310736 | tf_op jit(solution)/shard_map/all_gather | solution.py:16
  276.5 8.7 %while.61 = (s32[]{:T(128)}, f32[16,2560]{1,0:T(8,128)S(1)}, s32[]{:T(128)}, f32[8,2560]{1,0:T(8,128)S(1)}, f32[16,2560]{1,0:T(8,128)S(1)}, /*index=5*/f32[8,16,2560]{2,1,0:T(8,128)}, s32[]{:T(128)}, s32[]{:T(128)}) while((s32[]{:T(128)}, f32[16,2560]{1,0:T(8,128)S(1)}, s32[]{:T(128)}, f32[8,2560]{1,0:T(8,128)S(1)}, ...), condition=%wide.region_27.28_spmd.clone, body=%wide.region_26.27_spmd.clone.sunk | while | flops 204804 | bytes 686193 | solution.py:28
  285.9 7.1 %fusion.44 = bf16[1,128,2560]{2,1,0:T(8,128)(2,1)S(1)} fusion(f32[2560]{0:T(1024)S(1)} %copy-done.36, f32[2560]{0:T(1024)S(1)} %get-tuple-element.567, f32[2560]{0:T(1024)S(1)} %copy-done.34, f32[128]{0:T(128)S(1)} %get-tuple-element.722, f32[2560]{0:T(1024)S(1)} %get-tuple-element.568, f32[2560]{0:T(1024)S(1)} %copy-done.35, ...), kind=kLoop, calls=%fused_computation.178 | loop fusion | flops 26869760 | bytes 8916992 | tf_op jit(solution)/shard_map/stack | solution.py:136
  (729 shorter events, 131.4 us)
Async XLA Ops:
  6.5 10.8 %copy-start = (bf16[1,2560,192]{1,2,0:T(8,128)(2,1)S(1)}, bf16[1,2560,192]{1,2,0:T(8,128)(2,1)}, u32[]{:S(2)}) copy-start(bf16[1,2560,192]{1,2,0:T(8,128)(2,1)} %param.23) | copy-start | bytes 2949124
  6.5 10.5 %copy-start.6 = (bf16[1,128,2560]{2,1,0:T(8,128)(2,1)S(1)}, bf16[1,128,2560]{2,1,0:T(8,128)(2,1)}, u32[]{:S(2)}) copy-start(bf16[1,128,2560]{2,1,0:T(8,128)(2,1)} %param.18) | copy-start | bytes 1966084
  6.5 125.2 %all-gather.7.cloned.1.call-start = ((), (), s32[]{:S(2)}) async-start(), calls=%async_computation | async-start | bytes 1474560 | tf_op jit(solution)/shard_map/all_gather | solution.py:16
  7.5 8.2 %collective-permute-start = (bf16[3,2560]{1,0:T(4,128)(2,1)S(1)}, bf16[3,2560]{1,0:T(4,128)(2,1)S(1)}, u32[]{:S(2)}, u32[]{:S(2)}) collective-permute-start(bf16[3,2560]{1,0:T(4,128)(2,1)S(1)} %slice_bitcast_fusion.32), channel_id=1, source_target_pairs={{0,1},{1,2},{2,3},{3,4},{4,5},{5,6},{6,7},{8,9},{9,10},{10,11},{11... | collective-permute-start | bytes 46088 | tf_op jit(solution)/shard_map/ppermute | solution.py:34
  13.3 6.1 %copy-start.9 = (f32[2560]{0:T(1024)}, f32[2560]{0:T(1024)S(1)}, u32[]{:S(2)}) copy-start(f32[2560]{0:T(1024)S(1)} %get-tuple-element.602) | copy-start | bytes 30724
  22.8 71.3 %copy-start.39 = (f32[1,2560]{1,0:T(1,128)S(1)}, f32[1,2560]{1,0:T(1,128)}, u32[]{:S(2)}) copy-start(f32[1,2560]{1,0:T(1,128)} %param.27) | copy-start | bytes 30724
  88.6 187.8 %all-gather.9.cloned.1.call-start = ((), (), s32[]{:S(2)}) async-start(), calls=%async_computation.1 | async-start | bytes 1474560 | tf_op jit(solution)/shard_map/all_gather | solution.py:16
  90.0 63.3 %collective-permute-start.1 = (bf16[1,3,2560]{2,1,0:T(4,128)(2,1)}, bf16[1,3,2560]{2,1,0:T(4,128)(2,1)}, u32[]{:S(2)}, u32[]{:S(2)}) collective-permute-start(bf16[1,3,2560]{2,1,0:T(4,128)(2,1)} %slice.704), channel_id=1, source_target_pairs={{0,1},{1,2},{2,3},{3,4},{4,5},{5,6},{6,7},{8,9},{9,10},{10,11},{11... | collective-permute-start | bytes 46088 | tf_op jit(solution)/shard_map/ppermute | solution.py:34
  148.1 8.2 %copy-start.7 = (bf16[128,2560]{1,0:T(8,128)(2,1)}, bf16[128,2560]{1,0:T(8,128)(2,1)S(1)}, u32[]{:S(2)}) copy-start(bf16[128,2560]{1,0:T(8,128)(2,1)S(1)} %fusion.26) | copy-start | bytes 1966084
  148.1 5.2 %collective-permute-start.2 = (bf16[3,2560]{1,0:T(4,128)(2,1)S(1)}, bf16[3,2560]{1,0:T(4,128)(2,1)S(1)}, u32[]{:S(2)}, u32[]{:S(2)}) collective-permute-start(bf16[3,2560]{1,0:T(4,128)(2,1)S(1)} %slice.834), channel_id=1, source_target_pairs={{0,9},{1,10},{2,11},{3,12},{4,13},{5,14},{6,15},{7,16},{8,17},{9,1... | collective-permute-start | bytes 46088 | tf_op jit(solution)/shard_map/ppermute | solution.py:34
  149.5 5.3 %collective-permute-start.3 = (bf16[128,2560]{1,0:T(8,128)(2,1)S(1)}, bf16[128,2560]{1,0:T(8,128)(2,1)S(1)}, u32[]{:S(2)}, u32[]{:S(2)}) collective-permute-start(bf16[128,2560]{1,0:T(8,128)(2,1)S(1)} %fusion.26), channel_id=1, source_target_pairs={{0,8},{8,16},{16,24},{1,9},{9,17},{17,25},{2,10},{10,18},{18,26},{... | collective-permute-start | bytes 1966088 | tf_op jit(solution)/shard_map/ppermute | solution.py:34
  276.4 9.3 %copy-start.11 = (f32[2560]{0:T(1024)S(1)}, f32[2560]{0:T(1024)}, u32[]{:S(2)}) copy-start(f32[2560]{0:T(1024)} %copy-done.9) | copy-start | bytes 30724
  276.4 9.3 %copy-start.14 = (f32[2560]{0:T(1024)S(1)}, f32[2560]{0:T(1024)}, u32[]{:S(2)}) copy-start(f32[2560]{0:T(1024)} %copy-done.12) | copy-start | bytes 30724
  276.4 9.3 %copy-start.17 = (f32[2560]{0:T(1024)S(1)}, f32[2560]{0:T(1024)}, u32[]{:S(2)}) copy-start(f32[2560]{0:T(1024)} %copy-done.15) | copy-start | bytes 30724
  276.4 9.4 %copy-start.20 = (f32[2560]{0:T(1024)S(1)}, f32[2560]{0:T(1024)}, u32[]{:S(2)}) copy-start(f32[2560]{0:T(1024)} %get-tuple-element.569) | copy-start | bytes 30724
  276.4 9.4 %copy-start.21 = (f32[2560]{0:T(1024)S(1)}, f32[2560]{0:T(1024)}, u32[]{:S(2)}) copy-start(f32[2560]{0:T(1024)} %get-tuple-element.570) | copy-start | bytes 30724
  276.4 9.4 %copy-start.22 = (f32[2560]{0:T(1024)S(1)}, f32[2560]{0:T(1024)}, u32[]{:S(2)}) copy-start(f32[2560]{0:T(1024)} %get-tuple-element.571) | copy-start | bytes 30724
  276.4 9.4 %copy-start.23 = (f32[2560]{0:T(1024)S(1)}, f32[2560]{0:T(1024)}, u32[]{:S(2)}) copy-start(f32[2560]{0:T(1024)} %get-tuple-element.572) | copy-start | bytes 30724
  276.4 9.4 %copy-start.24 = (f32[2560]{0:T(1024)S(1)}, f32[2560]{0:T(1024)}, u32[]{:S(2)}) copy-start(f32[2560]{0:T(1024)} %get-tuple-element.573) | copy-start | bytes 30724
  276.4 9.4 %copy-start.25 = (f32[2560]{0:T(1024)S(1)}, f32[2560]{0:T(1024)}, u32[]{:S(2)}) copy-start(f32[2560]{0:T(1024)} %get-tuple-element.574) | copy-start | bytes 30724
  276.4 9.4 %copy-start.26 = (f32[2560]{0:T(1024)S(1)}, f32[2560]{0:T(1024)}, u32[]{:S(2)}) copy-start(f32[2560]{0:T(1024)} %get-tuple-element.575) | copy-start | bytes 30724
  276.4 9.4 %copy-start.27 = (f32[2560]{0:T(1024)S(1)}, f32[2560]{0:T(1024)}, u32[]{:S(2)}) copy-start(f32[2560]{0:T(1024)} %get-tuple-element.576) | copy-start | bytes 30724
  276.4 9.4 %copy-start.28 = (f32[2560]{0:T(1024)S(1)}, f32[2560]{0:T(1024)}, u32[]{:S(2)}) copy-start(f32[2560]{0:T(1024)} %get-tuple-element.577) | copy-start | bytes 30724
  276.4 9.4 %copy-start.29 = (f32[2560]{0:T(1024)S(1)}, f32[2560]{0:T(1024)}, u32[]{:S(2)}) copy-start(f32[2560]{0:T(1024)} %get-tuple-element.578) | copy-start | bytes 30724
  276.5 9.4 %copy-start.30 = (f32[2560]{0:T(1024)S(1)}, f32[2560]{0:T(1024)}, u32[]{:S(2)}) copy-start(f32[2560]{0:T(1024)} %get-tuple-element.579) | copy-start | bytes 30724
  276.5 9.4 %copy-start.31 = (f32[2560]{0:T(1024)S(1)}, f32[2560]{0:T(1024)}, u32[]{:S(2)}) copy-start(f32[2560]{0:T(1024)} %get-tuple-element.580) | copy-start | bytes 30724
  276.5 9.4 %copy-start.32 = (f32[2560]{0:T(1024)S(1)}, f32[2560]{0:T(1024)}, u32[]{:S(2)}) copy-start(f32[2560]{0:T(1024)} %get-tuple-element.581) | copy-start | bytes 30724
  276.5 9.4 %copy-start.33 = (f32[2560]{0:T(1024)S(1)}, f32[2560]{0:T(1024)}, u32[]{:S(2)}) copy-start(f32[2560]{0:T(1024)} %get-tuple-element.582) | copy-start | bytes 30724
  276.5 9.4 %copy-start.34 = (f32[2560]{0:T(1024)S(1)}, f32[2560]{0:T(1024)}, u32[]{:S(2)}) copy-start(f32[2560]{0:T(1024)} %get-tuple-element.583) | copy-start | bytes 30724
  276.5 9.4 %copy-start.35 = (f32[2560]{0:T(1024)S(1)}, f32[2560]{0:T(1024)}, u32[]{:S(2)}) copy-start(f32[2560]{0:T(1024)} %get-tuple-element.584) | copy-start | bytes 30724
  276.5 9.4 %copy-start.36 = (f32[2560]{0:T(1024)S(1)}, f32[2560]{0:T(1024)}, u32[]{:S(2)}) copy-start(f32[2560]{0:T(1024)} %reduce.73) | copy-start | bytes 30724
  285.9 7.1 %copy-start.8 = (bf16[128,2560]{1,0:T(8,128)(2,1)S(1)}, bf16[128,2560]{1,0:T(8,128)(2,1)}, u32[]{:S(2)}) copy-start(bf16[128,2560]{1,0:T(8,128)(2,1)} %copy-done.7) | copy-start | bytes 1966084
  (16 other events, 32.6 us)
Sparse Core Ops, SparseCore 0:
  88.7 42.4 all-gather.6
  228.1 48.2 all-gather.8
where the time goes:
time: 305 us; the launch traced here: 301 us
  other arithmetic  149 us (49%)
  blocking collectives  61.6 us (20%)
  local copies, waits for them, and re-layouts  40.1 us (13%)
  between operations  14.2 us (5%)
  starting transfers between devices  14.1 us (5%)
  waiting for transfers between devices  14.1 us (5%)
  loops' own time  4.42 us (1%)
  matrix products  3.99 us (1%)
    slice x32, other arithmetic, advance(): drive_blk[inner_t][None, :]  72.1 us
    all_gather x2, blocking collectives, prefix(): everything = jax.tree.map(lambda part: lax.all_gather(part, axis), shard)  61.6 us
    reduce_sum x96, other arithmetic, advance(): emitted.append(jnp.sum(c_blk[inner_t][:, None] * state, axis=0))  25.7 us
    dynamic_update_slice x32, local copies, waits for them, and re-layouts, token_scan(): final, outputs = lax.scan(advance, start, packed)  20.7 us
    select_n x16, other arithmetic, step(): return jax.tree.map(lambda a, b: jnp.where(reached, a, b), new, before)  16.4 us
    ppermute x4, starting transfers between devices, passed_along(): lax.ppermute(value, axis, [(source, source + steps) for source in range(i...  14.1 us
    all_gather x2, waiting for transfers between devices, prefix(): everything = jax.tree.map(lambda part: lax.all_gather(part, axis), shard)  13.3 us
    convert_element_type x1, other arithmetic, layer(): return (outputs + skip_w * inputs).astype(jnp.bfloat16)  7.22 us
  transfers between devices with their start and end apart: 6, of which 2 were waited for; matrix products, arithmetic and copies ran while one was open for 11% of the time, Pallas kernels for 0%

commit v1 on v0

v1 whole, which is shorter than its diff:
```python
import functools
import math

import jax
import jax.numpy as jnp
from jax import lax
from jax.experimental import pallas as pl
from jax.experimental.pallas import tpu as pltpu
from jax.sharding import PartitionSpec as P

STATE = 16
RANK = 160
KERNEL = 4
TICKS = 2
GROUP = 16
PAD = 8
LOG2E = math.log2(math.e)


def prefix(shard, axis, combine, identity):
    size, position = (lax.axis_size(axis), lax.axis_index(axis))
    everything = jax.tree.map(lambda part: lax.all_gather(part, axis), shard)
    start = jax.tree.map(
        lambda part, zero: jnp.broadcast_to(jnp.asarray(zero, part.dtype), part.shape),
        shard,
        identity,
    )

    def step(k, before):
        reached = k < position
        new = combine(before, jax.tree.map(lambda part: part[k], everything))
        return jax.tree.map(lambda a, b: jnp.where(reached, a, b), new, before)

    return lax.fori_loop(0, size, step, start)


def passed_along(value, axis, steps):
    count = lax.axis_size(axis)
    initial, last = (max(0, -steps), min(count, count - steps))
    return lax.ppermute(value, axis, [(source, source + steps) for source in range(initial, last)])


def pass_carries(totals, ends, rates):

    def link(earlier, later):
        return (earlier[0] + later[0], jnp.exp(-rates * later[0]) * earlier[1] + later[1])

    empty = (jnp.zeros_like(totals), jnp.zeros_like(ends))
    _, incoming = prefix((totals, ends), "seq", link, empty)
    return incoming


def tile_of(width):
    return next(tile for tile in (512, 256, 128, width) if width % tile == 0)


def block_diagonal(cmat):
    rows = cmat.shape[0]
    wide = GROUP * STATE
    pick = lax.broadcasted_iota(jnp.int32, (STATE, wide), 0) == lax.broadcasted_iota(jnp.int32, (STATE, wide), 1) % STATE
    spread = jnp.dot(cmat.astype(jnp.bfloat16), pick.astype(jnp.bfloat16), preferred_element_type=jnp.float32)
    own = lax.broadcasted_iota(jnp.int32, (rows, wide), 0) % GROUP == lax.broadcasted_iota(jnp.int32, (rows, wide), 1) // STATE
    return jnp.where(own, spread, 0.0).astype(jnp.bfloat16)


def scan_kernel(cur, before, gain, conv_w, conv_b, x_w, dt_w, dt_b, rates, skip_w,
                out, ends, summed, cblk, normed, mixed, steps, drive, bwide, hist):
    rows, width = cur.shape
    tile = tile_of(width)
    tiles = width // tile
    groups = rows // GROUP

    def norm(rows_bf):
        values = rows_bf.astype(jnp.float32)
        return values * lax.rsqrt(jnp.mean(values * values, axis=-1, keepdims=True) + 1e-05) * gain[...]

    normed[pl.ds(0, PAD), :] = norm(before[...])

    @pl.loop(0, rows // 16)
    def _(g):
        at = pl.multiple_of(g * 16, 16)
        normed[pl.ds(pl.multiple_of(at + PAD, PAD), 16), :] = norm(cur[pl.ds(at, 16), :])

    @pl.loop(0, tiles)
    def _(c):
        cols = pl.ds(pl.multiple_of(c * tile, tile), tile)
        conv = jnp.broadcast_to(conv_b[:, cols], (rows, tile))
        for k in range(KERNEL):
            conv = conv + conv_w[k:k + 1, cols].astype(jnp.float32) * normed[PAD - KERNEL + 1 + k:PAD - KERNEL + 1 + k + rows, cols]
        mixed[:, cols] = (conv * jax.nn.sigmoid(conv)).astype(jnp.bfloat16)

    proj = jnp.dot(mixed[...], x_w[...], preferred_element_type=jnp.float32)
    dt_low = proj[:, :RANK].astype(jnp.bfloat16)
    bmat = proj[:, RANK:RANK + STATE]
    cmat = proj[:, RANK + STATE:]
    cblk[...] = block_diagonal(cmat)
    bcols = bmat.T
    for t in range(rows):
        bwide[t] = jnp.broadcast_to(bcols[:, t:t + 1], (STATE, 128))
    lower = (lax.broadcasted_iota(jnp.int32, (rows, rows), 0) >= lax.broadcasted_iota(jnp.int32, (rows, rows), 1)).astype(jnp.bfloat16)

    @pl.loop(0, tiles)
    def _(c):
        cols = pl.ds(pl.multiple_of(c * tile, tile), tile)
        raw = jnp.dot(dt_low, dt_w[:, cols], preferred_element_type=jnp.float32) + dt_b[:, cols]
        step = jnp.maximum(raw, 0.0) + jnp.log1p(jnp.exp(-jnp.abs(raw)))
        steps[:, cols] = step
        drive[:, cols] = step * mixed[:, cols].astype(jnp.float32)
        high = step.astype(jnp.bfloat16)
        low = (step - high.astype(jnp.float32)).astype(jnp.bfloat16)
        summed[:, cols] = jnp.dot(lower, high, preferred_element_type=jnp.float32) + jnp.dot(lower, low, preferred_element_type=jnp.float32)

    @pl.loop(0, tiles)
    def _(c):
        cols = pl.ds(pl.multiple_of(c * tile, tile), tile)
        decay = rates[:, cols] * (-LOG2E)

        def emit(g):
            span = pl.ds(pl.multiple_of(g * GROUP, GROUP), GROUP)
            past = hist[pl.ds(pl.multiple_of(g * GROUP * STATE, GROUP * STATE), GROUP * STATE), :]
            local = jnp.dot(cblk[span, :], past, preferred_element_type=jnp.float32)
            out[span, cols] = local + skip_w[:, cols] * mixed[span, cols].astype(jnp.float32)

        def group(g, state):
            emit(jnp.maximum(g - 1, 0))
            at = pl.multiple_of(g * GROUP, GROUP)
            step_blk = steps[pl.ds(at, GROUP), cols]
            drive_blk = drive[pl.ds(at, GROUP), cols]
            for i in range(GROUP):
                b_row = jnp.concatenate([bwide[at + i]] * (tile // 128), axis=1)
                state = jnp.exp2(step_blk[i:i + 1] * decay) * state + b_row * drive_blk[i:i + 1]
                hist[pl.ds(pl.multiple_of((at + i) * STATE, STATE), STATE), :] = state.astype(jnp.bfloat16)
            return state

        ends[:, cols] = lax.fori_loop(0, groups, group, jnp.zeros((STATE, tile), jnp.float32))
        emit(groups - 1)


def fix_kernel(local, summed, cblk, incoming, rates, out, hist):
    rows, width = local.shape
    tile = tile_of(width)
    groups = rows // GROUP

    @pl.loop(0, width // tile)
    def _(c):
        cols = pl.ds(pl.multiple_of(c * tile, tile), tile)
        decay = rates[:, cols] * (-LOG2E)
        start = incoming[:, cols]

        def emit(g):
            span = pl.ds(pl.multiple_of(g * GROUP, GROUP), GROUP)
            past = hist[pl.ds(pl.multiple_of(g * GROUP * STATE, GROUP * STATE), GROUP * STATE), :]
            fixed = jnp.dot(cblk[span, :], past, preferred_element_type=jnp.float32)
            out[span, cols] = (local[span, cols] + fixed).astype(out.dtype)

        @pl.loop(0, groups)
        def _(g):
            emit(jnp.maximum(g - 1, 0))
            at = pl.multiple_of(g * GROUP, GROUP)
            sum_blk = summed[pl.ds(at, GROUP), cols]
            for i in range(GROUP):
                moved = jnp.exp2(sum_blk[i:i + 1] * decay) * start
                hist[pl.ds(pl.multiple_of((at + i) * STATE, STATE), STATE), :] = moved.astype(jnp.bfloat16)

        emit(groups - 1)


VMEM = pl.BlockSpec(memory_space=pltpu.VMEM)


def layer(current, before, gain, conv_w, conv_b, x_w, dt_w, dt_b, rates, skip_w):
    rows, width = current.shape
    tile = tile_of(width)
    f32, bf16 = jnp.float32, jnp.bfloat16
    local, ends, summed, cblk = pl.pallas_call(
        scan_kernel,
        out_shape=(
            jax.ShapeDtypeStruct((rows, width), f32),
            jax.ShapeDtypeStruct((STATE, width), f32),
            jax.ShapeDtypeStruct((rows, width), f32),
            jax.ShapeDtypeStruct((rows, GROUP * STATE), bf16),
        ),
        in_specs=[VMEM] * 10,
        out_specs=(VMEM,) * 4,
        scratch_shapes=[
            pltpu.VMEM((rows + PAD, width), f32),
            pltpu.VMEM((rows, width), bf16),
            pltpu.VMEM((rows, width), f32),
            pltpu.VMEM((rows, width), f32),
            pltpu.VMEM((rows, STATE, 128), f32),
            pltpu.VMEM((rows * STATE, tile), bf16),
        ],
        compiler_params=pltpu.CompilerParams(vmem_limit_bytes=40 << 20),
        name="local_scan",
    )(current, before, gain, conv_w, conv_b, x_w, dt_w, dt_b, rates, skip_w)
    incoming = pass_carries(summed[-1:], ends, rates)
    return pl.pallas_call(
        fix_kernel,
        out_shape=jax.ShapeDtypeStruct((rows, width), bf16),
        in_specs=[VMEM] * 5,
        out_specs=VMEM,
        scratch_shapes=[pltpu.VMEM((rows * STATE, tile), bf16)],
        compiler_params=pltpu.CompilerParams(vmem_limit_bytes=40 << 20),
        name="carry_fix",
    )(local, summed, cblk, incoming, rates)


def local(acts, feed, norm_gain, conv_weight, conv_bias, x_proj, dt_proj, dt_bias, a_rate, skip):
    section_zero = lax.axis_index("section") == 0
    seq_zero = lax.axis_index("seq") == 0
    weights = (norm_gain, conv_weight[0], conv_bias, x_proj[0], dt_proj[0], dt_bias, a_rate[0], skip)
    current = acts[0]
    prev_now, prev_feeds = passed_along((acts[0][-PAD:], feed[:, -PAD:, :]), "seq", 1)
    results = []
    for tick in range(TICKS):
        result = layer(current, prev_now, *weights)
        results.append(result)
        if tick + 1 < TICKS:
            received = passed_along(result, "section", 1)
            current = jnp.where(section_zero, feed[tick], received)
            diagonal = passed_along(result[-PAD:], ("section", "seq"), lax.axis_size("seq") + 1)
            diagonal = jnp.where(seq_zero, jnp.zeros_like(diagonal), diagonal)
            prev_now = jnp.where(section_zero, prev_feeds[tick], diagonal)
    return jnp.stack(results, 0)[:, None]


def solution(mesh):
    return jax.shard_map(
        local,
        mesh=mesh,
        in_specs=(
            P("section", "seq", None),
            P(None, "seq", None),
            P("section", None),
            P("section", None, None),
            P("section", None),
            P("section", None, None),
            P("section", None, None),
            P("section", None),
            P("section", None, None),
            P("section", None),
        ),
        out_specs=P(None, "section", "seq", None),
        check_vma=False,
    )
```

time: 305 us -> 198 us (0.65)
  the two profiles are of different devices: /device:TPU:0 before, /device:TPU:28 now
where the time goes in v1:
time: 198 us; the launch traced here: 194 us
  blocking collectives  58.1 us (29%)
  Pallas kernels  46.8 us (24%)
  waiting for transfers between devices  31.5 us (16%)
  other arithmetic  18.8 us (9%)
  local copies, waits for them, and re-layouts  15.1 us (8%)
  between operations  13.6 us (7%)
  starting transfers between devices  9.79 us (5%)
    all_gather x2, blocking collectives, prefix(): everything = jax.tree.map(lambda part: lax.all_gather(part, axis), shard)  58.1 us
    pallas_call x2, Pallas kernels, layer(): pl.pallas_call(scan_kernel, out_shape=(jax.ShapeDtypeStruct((rows, width)...  30.6 us
    all_gather x2, waiting for transfers between devices, prefix(): everything = jax.tree.map(lambda part: lax.all_gather(part, axis), shard)  19.3 us
    select_n x16, other arithmetic, step(): return jax.tree.map(lambda a, b: jnp.where(reached, a, b), new, before)  16.4 us
    pallas_call x2, Pallas kernels, layer(): pl.pallas_call(fix_kernel, out_shape=jax.ShapeDtypeStruct((rows, width),...  16.2 us
    unnamed x35, local copies, waits for them, and re-layouts  12.8 us
    ppermute x4, waiting for transfers between devices, passed_along(): lax.ppermute(value, axis, [(source, source + steps) for source in range(i...  12.1 us
    ppermute x4, starting transfers between devices, passed_along(): lax.ppermute(value, axis, [(source, source + steps) for source in range(i...  9.71 us
  transfers between devices with their start and end apart: 6, of which 5 were waited for; matrix products, arithmetic and copies ran while one was open for 7% of the time, Pallas kernels for 4%

profile of v1, /device:TPU:28, one launch (start us, length us, event | category | flops | bytes accessed | tf_op | source)
XLA Modules:
  0.0 194.0 jit_solution(15703613678444277844)
XLA Ops:
  7.5 3.4 %collective-permute-start = (bf16[8,2560]{1,0:T(8,128)(2,1)S(1)}, bf16[8,2560]{1,0:T(8,128)(2,1)S(1)}, u32[]{:S(2)}, u32[]{:S(2)}) collective-permute-start(bf16[8,2560]{1,0:T(8,128)(2,1)S(1)} %slice_bitcast_fusion), channel_id=1, source_target_pairs={{0,1},{1,2},{2,3},{3,4},{4,5},{5,6},{6,7},{8,9},{9,10},{10,11},{11... | collective-permute-start | bytes 122888 | tf_op jit(solution)/shard_map/ppermute | solution.py:40
  10.9 1.5 copy.13
  12.5 1.8 collective-permute-done.before
  14.4 15.3 %local_scan.2 = (f32[128,2560]{1,0:T(8,128)S(1)}, f32[16,2560]{1,0:T(8,128)}, f32[128,2560]{1,0:T(8,128)S(1)}, bf16[128,256]{1,0:T(8,128)(2,1)S(1)}) custom-call(bf16[128,2560]{1,0:T(8,128)(2,1)S(1)} %bitcast.46, bf16[8,2560]{1,0:T(8,128)(2,1)S(1)} %collective-permute-done.before, f32[1,2560]{1,0:T(1,128)S(1)} %copy-done.12, bf16[4,2560]{1,0:T(4,128)(2,1)S(1)} %bitcast.47, ...), custom_call_target="tpu_custom_call" | custom-call | tf_op jit(solution)/shard_map/local_scan/pallas_call | solution.py:175
  29.7 1.1 copy-done.2
  30.7 1.1 copy-done.6
  32.7 2.5 %collective-permute-start.2 = (bf16[1,8,2560]{2,1,0:T(8,128)(2,1)S(1)}, bf16[1,8,2560]{2,1,0:T(8,128)(2,1)S(1)}, u32[]{:S(2)}, u32[]{:S(2)}) collective-permute-start(bf16[1,8,2560]{2,1,0:T(8,128)(2,1)S(1)} %slice.21), channel_id=1, source_target_pairs={{0,1},{1,2},{2,3},{3,4},{4,5},{5,6},{6,7},{8,9},{9,10},{10,11},{11... | collective-permute-start | bytes 122888 | tf_op jit(solution)/shard_map/ppermute | solution.py:40
  36.1 28.2 %all-gather.4 = f32[8,1,2560]{2,1,0:T(1,128)S(1)} all-gather(f32[1,1,2560]{2,1,0:T(1,128)S(1)} %slice_bitcast_fusion.2), channel_id=2, replica_groups=mesh['section'=4,'seq'=8] {'seq'}, dimensions={0}, use_global_device_ids=true | all-gather | bytes 92160 | tf_op jit(solution)/shard_map/all_gather | solution.py:22
  64.3 8.6 %all-gather.9.cloned.1.call-done = f32[128,2560]{1,0:T(8,128)} async-done(((f32[16,2560]{1,0:T(8,128)}), f32[128,2560]{1,0:T(8,128)}) %all-gather.9.cloned.1.call-update) | async-done | bytes 1310736 | tf_op jit(solution)/shard_map/all_gather | solution.py:22
  73.0 8.7 %while.32 = (s32[]{:T(128)}, f32[16,2560]{1,0:T(8,128)S(1)}, s32[]{:T(128)}, f32[8,1,2560]{2,1,0:T(1,128)S(1)}, f32[16,2560]{1,0:T(8,128)S(1)}, /*index=5*/f32[8,16,2560]{2,1,0:T(8,128)}, s32[]{:T(128)}, s32[]{:T(128)}) while((s32[]{:T(128)}, f32[16,2560]{1,0:T(8,128)S(1)}, s32[]{:T(128)}, f32[8,1,2560]{2,1,0:T(1,128)S(1)}, ...), condition=%wide.region_1.2_spmd.clone, body=%wide.region_0.1_spmd.clone.sunk | while | flops 204804 | bytes 686193 | solution.py:34
  73.0 1.0 fusion.4
  74.1 1.0 fusion.4
  75.2 1.0 fusion.4
  76.3 1.0 fusion.4
  81.7 1.3 copy-done.3
  83.0 1.3 copy-done.7
  84.3 8.1 %carry_fix.2 = bf16[128,2560]{1,0:T(8,128)(2,1)S(1)} custom-call(f32[128,2560]{1,0:T(8,128)S(1)} %copy-done.7, f32[128,2560]{1,0:T(8,128)S(1)} %copy-done.3, bf16[128,256]{1,0:T(8,128)(2,1)S(1)} %get-tuple-element.313.cblk, f32[16,2560]{1,0:T(8,128)S(1)} %get-tuple-element.315.incoming, f32[16,2560]{1,0:T(8,128)S(1)} %bitcast.39), custom_call_target="tpu_custom_call" | custom-call | tf_op jit(solution)/shard_map/carry_fix/pallas_call | solution.py:197
  92.4 1.9 collective-permute-start.3
  94.4 1.9 collective-permute-start.1
  96.3 3.3 %collective-permute-done.3 = bf16[8,2560]{1,0:T(8,128)(2,1)S(1)} collective-permute-done((bf16[8,2560]{1,0:T(8,128)(2,1)S(1)}, bf16[8,2560]{1,0:T(8,128)(2,1)S(1)}, u32[]{:S(2)}, u32[]{:S(2)}) %collective-permute-start.3) | collective-permute-done | bytes 40992 | tf_op jit(solution)/shard_map/ppermute | solution.py:40
  99.6 7.0 %collective-permute-done.1 = bf16[128,2560]{1,0:T(8,128)(2,1)S(1)} collective-permute-done((bf16[128,2560]{1,0:T(8,128)(2,1)S(1)}, bf16[128,2560]{1,0:T(8,128)(2,1)S(1)}, u32[]{:S(2)}, u32[]{:S(2)}) %collective-permute-start.1) | collective-permute-done | bytes 655392 | tf_op jit(solution)/shard_map/ppermute | solution.py:40
  106.6 1.2 bitcast_select_fusion.cur
  107.7 15.3 %local_scan.3 = (f32[128,2560]{1,0:T(8,128)S(1)}, f32[16,2560]{1,0:T(8,128)}, f32[128,2560]{1,0:T(8,128)S(1)}, bf16[128,256]{1,0:T(8,128)(2,1)S(1)}) custom-call(bf16[128,2560]{1,0:T(8,128)(2,1)S(1)} %bitcast_select_fusion.cur, bf16[8,2560]{1,0:T(8,128)(2,1)S(1)} %bitcast_select_fusion.1.before, f32[1,2560]{1,0:T(1,128)S(1)} %copy-done.12, ...), custom_call_target="tpu_custom_call" | custom-call | tf_op jit(solution)/shard_map/local_scan/pallas_call | solution.py:175
  123.0 1.1 copy-done.4
  124.1 1.1 copy-done.8
  126.1 29.8 %all-gather.5 = f32[8,1,2560]{2,1,0:T(1,128)S(1)} all-gather(f32[1,1,2560]{2,1,0:T(1,128)S(1)} %slice_bitcast_fusion.1), channel_id=4, replica_groups=mesh['section'=4,'seq'=8] {'seq'}, dimensions={0}, use_global_device_ids=true | all-gather | bytes 92160 | tf_op jit(solution)/shard_map/all_gather | solution.py:22
  155.9 10.7 %all-gather.11.cloned.1.call-done = f32[128,2560]{1,0:T(8,128)} async-done(((f32[16,2560]{1,0:T(8,128)}), f32[128,2560]{1,0:T(8,128)}) %all-gather.11.cloned.1.call-update) | async-done | bytes 1310736 | tf_op jit(solution)/shard_map/all_gather | solution.py:22
  166.6 8.7 %while.33 = (s32[]{:T(128)}, f32[16,2560]{1,0:T(8,128)S(1)}, s32[]{:T(128)}, f32[8,1,2560]{2,1,0:T(1,128)S(1)}, f32[16,2560]{1,0:T(8,128)S(1)}, /*index=5*/f32[8,16,2560]{2,1,0:T(8,128)}, s32[]{:T(128)}, s32[]{:T(128)}) while((s32[]{:T(128)}, f32[16,2560]{1,0:T(8,128)S(1)}, s32[]{:T(128)}, f32[8,1,2560]{2,1,0:T(1,128)S(1)}, ...), condition=%wide.region_3.4_spmd.clone, body=%wide.region_2.3_spmd.clone.sunk | while | flops 204804 | bytes 686193 | solution.py:34
  175.3 1.3 copy-done.5
  176.6 1.3 copy-done.9
  177.9 8.1 %carry_fix.3 = bf16[128,2560]{1,0:T(8,128)(2,1)S(1)} custom-call(f32[128,2560]{1,0:T(8,128)S(1)} %copy-done.9, f32[128,2560]{1,0:T(8,128)S(1)} %copy-done.5, bf16[128,256]{1,0:T(8,128)(2,1)S(1)} %get-tuple-element.318.cblk, f32[16,2560]{1,0:T(8,128)S(1)} %get-tuple-element.320.incoming, f32[16,2560]{1,0:T(8,128)S(1)} %bitcast.41), custom_call_target="tpu_custom_call" | custom-call | tf_op jit(solution)/shard_map/carry_fix/pallas_call | solution.py:197
  186.0 1.2 maximum_bitcast_fusion
  (66 shorter events, 16.5 us)
Async XLA Ops:
  6.5 7.8 %copy-start.10 = (bf16[1,128,2560]{2,1,0:T(8,128)(2,1)S(1)}, bf16[1,128,2560]{2,1,0:T(8,128)(2,1)}, u32[]{:S(2)}) copy-start(bf16[1,128,2560]{2,1,0:T(8,128)(2,1)} %param.14) | copy-start | bytes 1966084
  6.5 7.8 %copy-start = (f32[1,16,2560]{2,1,0:T(8,128)S(1)}, f32[1,16,2560]{2,1,0:T(8,128)}, u32[]{:S(2)}) copy-start(f32[1,16,2560]{2,1,0:T(8,128)} %param.22) | copy-start | bytes 491524
  6.5 7.8 %copy-start.11 = (bf16[1,4,2560]{2,1,0:T(4,128)(2,1)S(1)}, bf16[1,4,2560]{2,1,0:T(4,128)(2,1)}, u32[]{:S(2)}) copy-start(bf16[1,4,2560]{2,1,0:T(4,128)(2,1)} %param.17) | copy-start | bytes 61444
  6.5 7.8 %copy-start.1 = (bf16[1,160,2560]{2,1,0:T(8,128)(2,1)S(1)}, bf16[1,160,2560]{2,1,0:T(8,128)(2,1)}, u32[]{:S(2)}) copy-start(bf16[1,160,2560]{2,1,0:T(8,128)(2,1)} %param.20) | copy-start | bytes 2457604
  6.5 7.8 %copy-start.12 = (f32[1,2560]{1,0:T(1,128)S(1)}, f32[1,2560]{1,0:T(1,128)}, u32[]{:S(2)}) copy-start(f32[1,2560]{1,0:T(1,128)} %gain.3) | copy-start | bytes 30724
  6.5 7.8 %copy-start.13 = (f32[1,2560]{1,0:T(1,128)S(1)}, f32[1,2560]{1,0:T(1,128)}, u32[]{:S(2)}) copy-start(f32[1,2560]{1,0:T(1,128)} %conv_b.3) | copy-start | bytes 30724
  6.6 7.8 %copy-start.14 = (f32[1,2560]{1,0:T(1,128)S(1)}, f32[1,2560]{1,0:T(1,128)}, u32[]{:S(2)}) copy-start(f32[1,2560]{1,0:T(1,128)} %dt_b.3) | copy-start | bytes 30724
  6.6 7.8 %copy-start.15 = (f32[1,2560]{1,0:T(1,128)S(1)}, f32[1,2560]{1,0:T(1,128)}, u32[]{:S(2)}) copy-start(f32[1,2560]{1,0:T(1,128)} %skip_w.3) | copy-start | bytes 30724
  6.6 66.4 %all-gather.9.cloned.1.call-start = ((), (), s32[]{:S(2)}) async-start(), calls=%async_computation | async-start | bytes 1474560 | tf_op jit(solution)/shard_map/all_gather | solution.py:22
  7.5 6.8 %collective-permute-start = (bf16[8,2560]{1,0:T(8,128)(2,1)S(1)}, bf16[8,2560]{1,0:T(8,128)(2,1)S(1)}, u32[]{:S(2)}, u32[]{:S(2)}) collective-permute-start(bf16[8,2560]{1,0:T(8,128)(2,1)S(1)} %slice_bitcast_fusion), channel_id=1, source_target_pairs={{0,1},{1,2},{2,3},{3,4},{4,5},{5,6},{6,7},{8,9},{9,10},{10,11},{11... | collective-permute-start | bytes 122888 | tf_op jit(solution)/shard_map/ppermute | solution.py:40
  29.7 1.1 copy-start.2
  30.7 1.1 copy-start.6
  31.8 134.8 %all-gather.11.cloned.1.call-start = ((), (), s32[]{:S(2)}) async-start(), calls=%async_computation.1 | async-start | bytes 1474560 | tf_op jit(solution)/shard_map/all_gather | solution.py:22
  32.7 63.6 %collective-permute-start.2 = (bf16[1,8,2560]{2,1,0:T(8,128)(2,1)S(1)}, bf16[1,8,2560]{2,1,0:T(8,128)(2,1)S(1)}, u32[]{:S(2)}, u32[]{:S(2)}) collective-permute-start(bf16[1,8,2560]{2,1,0:T(8,128)(2,1)S(1)} %slice.21), channel_id=1, source_target_pairs={{0,1},{1,2},{2,3},{3,4},{4,5},{5,6},{6,7},{8,9},{9,10},{10,11},{11... | collective-permute-start | bytes 122888 | tf_op jit(solution)/shard_map/ppermute | solution.py:40
  81.7 1.3 copy-start.3
  83.0 1.3 copy-start.7
  92.4 7.1 %collective-permute-start.3 = (bf16[8,2560]{1,0:T(8,128)(2,1)S(1)}, bf16[8,2560]{1,0:T(8,128)(2,1)S(1)}, u32[]{:S(2)}, u32[]{:S(2)}) collective-permute-start(bf16[8,2560]{1,0:T(8,128)(2,1)S(1)} %slice.24), channel_id=1, source_target_pairs={{0,9},{1,10},{2,11},{3,12},{4,13},{5,14},{6,15},{7,16},{8,17},{9,1... | collective-permute-start | bytes 122888 | tf_op jit(solution)/shard_map/ppermute | solution.py:40
  94.4 12.2 %collective-permute-start.1 = (bf16[128,2560]{1,0:T(8,128)(2,1)S(1)}, bf16[128,2560]{1,0:T(8,128)(2,1)S(1)}, u32[]{:S(2)}, u32[]{:S(2)}) collective-permute-start(bf16[128,2560]{1,0:T(8,128)(2,1)S(1)} %carry_fix.2), channel_id=1, source_target_pairs={{0,8},{8,16},{16,24},{1,9},{9,17},{17,25},{2,10},{10,18},{18,26},{... | collective-permute-start | bytes 1966088 | tf_op jit(solution)/shard_map/ppermute | solution.py:40
  123.0 1.1 copy-start.4
  124.1 1.1 copy-start.8
  175.3 1.3 copy-start.5
  176.6 1.3 copy-start.9
Sparse Core Ops, SparseCore 0:
  31.9 40.9 all-gather.8
  125.3 41.2 all-gather.10

commit v2 on v1

--- a/solution.py
+++ b/solution.py
@@ -15,6 +15,8 @@
 GROUP = 16
 PAD = 8
 LOG2E = math.log2(math.e)
+MESH = pl.DeviceIdType.MESH
+VMEM = pl.BlockSpec(memory_space=pltpu.VMEM)
 
 
 def prefix(shard, axis, combine, identity):
@@ -48,6 +50,124 @@
     empty = (jnp.zeros_like(totals), jnp.zeros_like(ends))
     _, incoming = prefix((totals, ends), "seq", link, empty)
     return incoming
+
+
+def relay_kernel(ends, totals, rates, incoming, pend, ptot, hin, hout, pairs, decays,
+                 pend_send, pend_recv, tot_send, tot_recv, hin_recv, odd_send, even_send, *, size):
+    me = lax.axis_index("seq")
+    odd = lax.rem(me, 2) == 1
+    chunks, _, tile = pend.shape
+    later = jnp.logical_and(odd, me + 2 < size)
+    earlier = me > 1
+    barrier = pltpu.get_barrier_semaphore()
+
+    def greet(where):
+        pl.semaphore_signal(barrier, inc=1, device_id={"seq": where}, device_id_type=MESH)
+
+    def cols(j):
+        return pl.ds(j * tile, tile)
+
+    def to_pair(j):
+        return pltpu.make_async_remote_copy(ends.at[:, cols(j)], pend.at[j], pend_send.at[j], pend_recv.at[j],
+                                            device_id={"seq": me + 1}, device_id_type=MESH)
+
+    def to_pair_totals():
+        return pltpu.make_async_remote_copy(totals, ptot, tot_send, tot_recv,
+                                            device_id={"seq": me + 1}, device_id_type=MESH)
+
+    def to_odd(j):
+        return pltpu.make_async_remote_copy(hout.at[j], hin.at[j], odd_send.at[j], hin_recv.at[j],
+                                            device_id={"seq": me + 2}, device_id_type=MESH)
+
+    def to_even(j):
+        return pltpu.make_async_remote_copy(hout.at[j], hin.at[j], even_send.at[j], hin_recv.at[j],
+                                            device_id={"seq": me + 1}, device_id_type=MESH)
+
+    @pl.when(me > 0)
+    def _():
+        greet(me - 1)
+
+    @pl.when(jnp.logical_and(odd, earlier))
+    def _():
+        greet(me - 2)
+
+    @pl.when(jnp.logical_not(odd))
+    def _():
+        pl.semaphore_wait(barrier, 1)
+        to_pair_totals().start()
+        for j in range(chunks):
+            to_pair(j).start()
+
+    @pl.when(later)
+    def _():
+        pl.semaphore_wait(barrier, 2)
+
+    @pl.when(odd)
+    def _():
+        to_pair_totals().wait_recv()
+        for j in range(chunks):
+            at = cols(j)
+            scale = rates[:, at] * (-LOG2E)
+            decays[j] = jnp.exp2(scale * (ptot[:, at] + totals[:, at]))
+            to_pair(j).wait_recv()
+            pairs[j] = jnp.exp2(scale * totals[:, at]) * pend[j] + ends[:, at]
+
+    @pl.when(jnp.logical_not(earlier))
+    def _():
+        hin[...] = jnp.zeros_like(hin)
+
+    for j in range(chunks):
+        @pl.when(earlier)
+        def _():
+            to_odd(j).wait_recv()
+
+        @pl.when(later)
+        def _():
+            hout[j] = decays[j] * hin[j] + pairs[j]
+            to_odd(j).start()
+            to_even(j).start()
+
+    @pl.when(odd)
+    def _():
+        for j in range(chunks):
+            at = cols(j)
+            incoming[:, at] = jnp.exp2(rates[:, at] * (-LOG2E) * ptot[:, at]) * hin[j] + pend[j]
+
+    @pl.when(jnp.logical_not(odd))
+    def _():
+        for j in range(chunks):
+            incoming[:, cols(j)] = hin[j]
+        to_pair_totals().wait_send()
+        for j in range(chunks):
+            to_pair(j).wait_send()
+
+    @pl.when(later)
+    def _():
+        for j in range(chunks):
+            to_odd(j).wait_send()
+            to_even(j).wait_send()
+
+
+def relay_carries(totals, ends, rates):
+    size = lax.axis_size("seq")
+    if size % 2:
+        return pass_carries(totals, ends, rates)
+    width = ends.shape[1]
+    tile = tile_of(width)
+    chunks = width // tile
+    f32 = jnp.float32
+    slots = pltpu.VMEM((chunks, STATE, tile), f32)
+    each = pltpu.SemaphoreType.DMA((chunks,))
+    return pl.pallas_call(
+        functools.partial(relay_kernel, size=size),
+        out_shape=jax.ShapeDtypeStruct((STATE, width), f32),
+        in_specs=[VMEM] * 3,
+        out_specs=VMEM,
+        scratch_shapes=[slots, pltpu.VMEM((1, width), f32), slots, slots, slots, slots,
+                        each, each, pltpu.SemaphoreType.DMA, pltpu.SemaphoreType.DMA, each, each, each],
+        compiler_params=pltpu.CompilerParams(collective_id=0, has_side_effects=True, vmem_limit_bytes=16 << 20),
+        name="carry_relay",
+    )(ends, totals, rates)
 
 
 def tile_of(width):
@@ -163,9 +283,6 @@
                 hist[pl.ds(pl.multiple_of((at + i) * STATE, STATE), STATE), :] = moved.astype(jnp.bfloat16)
 
         emit(groups - 1)
-
-
-VMEM = pl.BlockSpec(memory_space=pltpu.VMEM)
 
 
 def layer(current, before, gain, conv_w, conv_b, x_w, dt_w, dt_b, rates, skip_w):
@@ -193,7 +310,7 @@
         compiler_params=pltpu.CompilerParams(vmem_limit_bytes=40 << 20),
         name="local_scan",
     )(current, before, gain, conv_w, conv_b, x_w, dt_w, dt_b, rates, skip_w)
-    incoming = pass_carries(summed[-1:], ends, rates)
+    incoming = relay_carries(summed[-1:], ends, rates)
     return pl.pallas_call(
         fix_kernel,
         out_shape=jax.ShapeDtypeStruct((rows, width), bf16),

time: 198 us -> 104 us (0.53); the launches traced: 194 us -> 104 us
  blocking collectives: 58.1 us -> 0 us
  Pallas kernels: 46.8 us -> 78.4 us
  waiting for transfers between devices: 31.5 us -> 10.3 us
  other arithmetic: 18.8 us -> 2.37 us
  between operations: 13.6 us -> 0.21 us
  local copies, waits for them, and re-layouts: 15.1 us -> 3.29 us
    all_gather x2 -> x0, blocking collectives: 58.1 us -> none  [prefix(): everything = jax.tree.map(lambda part: lax.all_gather(part, axis), shard)]
    pallas_call x0 -> x2, Pallas kernels: none -> 32.7 us  [relay_carries(): pl.pallas_call(functools.partial(relay_kernel, size=size), out_shape=jax....]
    all_gather x2 -> x0, waiting for transfers between devices: 19.3 us -> none  [prefix(): everything = jax.tree.map(lambda part: lax.all_gather(part, axis), shard)]
    select_n x16 -> x0, other arithmetic: 16.4 us -> none  [step(): return jax.tree.map(lambda a, b: jnp.where(reached, a, b), new, before)]
    unnamed x35 -> x17, local copies, waits for them, and re-layouts: 12.8 us -> 1.57 us
  transfers between devices with their start and end apart: 6 -> 4, of which waited for: 5 -> 2; matrix products, arithmetic and copies ran while one was open for 7% -> 2% of each run, Pallas kernels for 4% -> 41%
where the time goes in v2:
time: 104 us
  Pallas kernels  78.4 us (75%)
  waiting for transfers between devices  10.3 us (10%)
  starting transfers between devices  9.14 us (9%)
  local copies, waits for them, and re-layouts  3.29 us (3%)
  other arithmetic  2.37 us (2%)
    pallas_call x2, Pallas kernels, relay_carries(): pl.pallas_call(functools.partial(relay_kernel, size=size), out_shape=jax....  32.7 us
    pallas_call x2, Pallas kernels, layer(): pl.pallas_call(scan_kernel, out_shape=(jax.ShapeDtypeStruct((rows, width)...  29.5 us
    pallas_call x2, Pallas kernels, layer(): pl.pallas_call(fix_kernel, out_shape=jax.ShapeDtypeStruct((rows, width),...  16.2 us
    ppermute x4, waiting for transfers between devices, passed_along(): lax.ppermute(value, axis, [(source, source + steps) for source in range(i...  10.3 us
    ppermute x4, starting transfers between devices, passed_along(): lax.ppermute(value, axis, [(source, source + steps) for source in range(i...  9.14 us
  transfers between devices with their start and end apart: 4, of which 2 were waited for; matrix products, arithmetic and copies ran while one was open for 2% of the time, Pallas kernels for 41%

profile of v2, /device:TPU:28, one launch (start us, length us, event | category | flops | bytes accessed | tf_op | source)
XLA Modules:
  0.0 103.6 jit_solution(13195597405160441123)
XLA Ops:
  0.0 0.0 copy-start.5
  0.0 0.0 copy-start.4
  0.0 0.0 copy-start
  0.0 0.0 copy-start.1
  0.0 0.0 copy-start.3
  0.1 0.9 slice_bitcast_fusion
  1.0 3.4 %collective-permute-start = (bf16[8,2560]{1,0:T(8,128)(2,1)S(1)}, bf16[8,2560]{1,0:T(8,128)(2,1)S(1)}, u32[]{:S(2)}, u32[]{:S(2)}) collective-permute-start(bf16[8,2560]{1,0:T(8,128)(2,1)S(1)} %slice_bitcast_fusion), channel_id=1, source_target_pairs={{0,1},{1,2},{2,3},{3,4},{4,5},{5,6},{6,7},{8,9},{9,10},{10,11},{11... | collective-permute-start | bytes 122888 | tf_op jit(solution)/shard_map/ppermute | solution.py:42
  4.3 0.8 slice.21
  5.1 1.9 %collective-permute-start.2 = (bf16[1,8,2560]{2,1,0:T(8,128)(2,1)S(1)}, bf16[1,8,2560]{2,1,0:T(8,128)(2,1)S(1)}, u32[]{:S(2)}, u32[]{:S(2)}) collective-permute-start(bf16[1,8,2560]{2,1,0:T(8,128)(2,1)S(1)} %slice.21), channel_id=1, source_target_pairs={{0,1},{1,2},{2,3},{3,4},{4,5},{5,6},{6,7},{8,9},{9,10},{10,11},{11... | collective-permute-start | bytes 122888 | tf_op jit(solution)/shard_map/ppermute | solution.py:42
  7.1 1.5 %copy.11 = bf16[1,2560,192]{2,1,0:T(8,128)(2,1)S(1)} copy(bf16[1,2560,192]{1,2,0:T(8,128)(2,1)} %param.15) | data formatting | bytes 1966080 | tf_op args[5]
  8.6 0.0 collective-permute-done.before
  8.6 0.0 copy-done.2
  8.6 0.0 copy-done.7
  8.6 0.0 copy-done.6
  8.6 0.0 copy-done.5
  8.6 0.0 copy-done.4
  8.7 0.0 copy-done
  8.7 0.0 copy-done.1
  8.7 0.0 copy-done.3
  8.7 14.8 %local_scan.2 = (f32[128,2560]{1,0:T(8,128)S(1)}, f32[16,2560]{1,0:T(8,128)S(1)}, f32[128,2560]{1,0:T(8,128)S(1)}, bf16[128,256]{1,0:T(8,128)(2,1)S(1)}) custom-call(bf16[128,2560]{1,0:T(8,128)(2,1)S(1)} %bitcast.29, bf16[8,2560]{1,0:T(8,128)(2,1)S(1)} %collective-permute-done.before, f32[1,2560]{1,0:T(1,128)S(1)} %copy-done.4, ...), custom_call_target="tpu_custom_call" | custom-call | tf_op jit(solution)/shard_map/local_scan/pallas_call | solution.py:292
  23.5 19.8 %carry_relay.2.incoming = f32[16,2560]{1,0:T(8,128)S(1)} custom-call(f32[16,2560]{1,0:T(8,128)S(1)} %get-tuple-element.16.ends, f32[1,2560]{1,0:T(1,128)S(1)} %slice.20.totals, f32[16,2560]{1,0:T(8,128)S(1)} %bitcast.20), custom_call_target="tpu_custom_call" | custom-call | tf_op jit(solution)/shard_map/carry_relay/pallas_call | solution.py:161
  43.3 8.1 %carry_fix.2 = bf16[128,2560]{1,0:T(8,128)(2,1)S(1)} custom-call(f32[128,2560]{1,0:T(8,128)S(1)} %get-tuple-element.13.local, f32[128,2560]{1,0:T(8,128)S(1)} %get-tuple-element.14.summed, bf16[128,256]{1,0:T(8,128)(2,1)S(1)} %get-tuple-element.15.cblk, f32[16,2560]{1,0:T(8,128)S(1)} %carry_relay.2.incoming, f32[16,2560]{1,0:T(8,128)S(1)} %bitcast.21), custom_call_target="tpu_custom_call" | custom-call | tf_op jit(solution)/shard_map/carry_fix/pallas_call | solution.py:314
  51.4 1.9 %collective-permute-start.3 = (bf16[8,2560]{1,0:T(8,128)(2,1)S(1)}, bf16[8,2560]{1,0:T(8,128)(2,1)S(1)}, u32[]{:S(2)}, u32[]{:S(2)}) collective-permute-start(bf16[8,2560]{1,0:T(8,128)(2,1)S(1)} %slice.24), channel_id=1, source_target_pairs={{0,9},{1,10},{2,11},{3,12},{4,13},{5,14},{6,15},{7,16},{8,17},{9,1... | collective-permute-start | bytes 122888 | tf_op jit(solution)/shard_map/ppermute | solution.py:42
  53.3 1.9 %collective-permute-start.1 = (bf16[128,2560]{1,0:T(8,128)(2,1)S(1)}, bf16[128,2560]{1,0:T(8,128)(2,1)S(1)}, u32[]{:S(2)}, u32[]{:S(2)}) collective-permute-start(bf16[128,2560]{1,0:T(8,128)(2,1)S(1)} %carry_fix.2), channel_id=1, source_target_pairs={{0,8},{8,16},{16,24},{1,9},{9,17},{17,25},{2,10},{10,18},{18,26},{... | collective-permute-start | bytes 1966088 | tf_op jit(solution)/shard_map/ppermute | solution.py:42
  55.2 0.0 collective-permute-done.2
  55.3 3.3 %collective-permute-done.3 = bf16[8,2560]{1,0:T(8,128)(2,1)S(1)} collective-permute-done((bf16[8,2560]{1,0:T(8,128)(2,1)S(1)}, bf16[8,2560]{1,0:T(8,128)(2,1)S(1)}, u32[]{:S(2)}, u32[]{:S(2)}) %collective-permute-start.3) | collective-permute-done | bytes 40992 | tf_op jit(solution)/shard_map/ppermute | solution.py:42
  58.5 7.0 %collective-permute-done.1 = bf16[128,2560]{1,0:T(8,128)(2,1)S(1)} collective-permute-done((bf16[128,2560]{1,0:T(8,128)(2,1)S(1)}, bf16[128,2560]{1,0:T(8,128)(2,1)S(1)}, u32[]{:S(2)}, u32[]{:S(2)}) %collective-permute-start.1) | collective-permute-done | bytes 655392 | tf_op jit(solution)/shard_map/ppermute | solution.py:42
  65.5 1.2 %bitcast_select_fusion.cur = bf16[128,2560]{1,0:T(8,128)(2,1)S(1)} fusion(bf16[128,2560]{1,0:T(8,128)(2,1)S(1)} %collective-permute-done.1, bf16[1,128,2560]{2,1,0:T(8,128)(2,1)} %param.11, pred[]{:T(512)S(6)} %eq.6), kind=kLoop, calls=%fused_computation.1 | loop fusion | flops 327680 | bytes 1966081 | tf_op jit(solution)/shard_map/jit(_where)/select_n | solution.py:337
  66.7 14.7 %local_scan.3 = (f32[128,2560]{1,0:T(8,128)S(1)}, f32[16,2560]{1,0:T(8,128)S(1)}, f32[128,2560]{1,0:T(8,128)S(1)}, bf16[128,256]{1,0:T(8,128)(2,1)S(1)}) custom-call(bf16[128,2560]{1,0:T(8,128)(2,1)S(1)} %bitcast_select_fusion.cur, bf16[8,2560]{1,0:T(8,128)(2,1)S(1)} %bitcast_select_fusion.1.before, f32[1,2560]{1,0:T(1,128)S(1)} %copy-done.4, ...), custom_call_target="tpu_custom_call" | custom-call | tf_op jit(solution)/shard_map/local_scan/pallas_call | solution.py:292
  81.5 12.9 %carry_relay.3.incoming = f32[16,2560]{1,0:T(8,128)S(1)} custom-call(f32[16,2560]{1,0:T(8,128)S(1)} %get-tuple-element.20.ends, f32[1,2560]{1,0:T(1,128)S(1)} %slice.23.totals, f32[16,2560]{1,0:T(8,128)S(1)} %bitcast.23), custom_call_target="tpu_custom_call" | custom-call | tf_op jit(solution)/shard_map/carry_relay/pallas_call | solution.py:161
  94.4 8.1 %carry_fix.3 = bf16[128,2560]{1,0:T(8,128)(2,1)S(1)} custom-call(f32[128,2560]{1,0:T(8,128)S(1)} %get-tuple-element.17.local, f32[128,2560]{1,0:T(8,128)S(1)} %get-tuple-element.18.summed, bf16[128,256]{1,0:T(8,128)(2,1)S(1)} %get-tuple-element.19.cblk, f32[16,2560]{1,0:T(8,128)S(1)} %carry_relay.3.incoming, f32[16,2560]{1,0:T(8,128)S(1)} %bitcast.24), custom_call_target="tpu_custom_call" | custom-call | tf_op jit(solution)/shard_map/carry_fix/pallas_call | solution.py:314
  102.4 1.2 %maximum_bitcast_fusion = bf16[2,1,128,2560]{3,2,1,0:T(8,128)(2,1)} fusion(bf16[1,128,2560]{2,1,0:T(8,128)(2,1)S(1)} %bitcast.28, bf16[1,128,2560]{2,1,0:T(8,128)(2,1)S(1)} %bitcast.27), kind=kLoop, calls=%fused_computation | loop fusion | flops 655360 | bytes 2621440 | tf_op jit(solution)/shard_map/broadcast_in_dim | solution.py:341
  (7 shorter events, 0.1 us)
Async XLA Ops:
  0.0 8.6 %copy-start.2 = (bf16[1,128,2560]{2,1,0:T(8,128)(2,1)S(1)}, bf16[1,128,2560]{2,1,0:T(8,128)(2,1)}, u32[]{:S(2)}) copy-start(bf16[1,128,2560]{2,1,0:T(8,128)(2,1)} %param.10) | copy-start | bytes 1966084
  0.0 8.6 %copy-start.7 = (f32[1,2560]{1,0:T(1,128)S(1)}, f32[1,2560]{1,0:T(1,128)}, u32[]{:S(2)}) copy-start(f32[1,2560]{1,0:T(1,128)} %skip_w.3) | copy-start | bytes 30724
  0.0 8.6 %copy-start.6 = (f32[1,2560]{1,0:T(1,128)S(1)}, f32[1,2560]{1,0:T(1,128)}, u32[]{:S(2)}) copy-start(f32[1,2560]{1,0:T(1,128)} %dt_b.3) | copy-start | bytes 30724
  0.0 8.6 %copy-start.5 = (f32[1,2560]{1,0:T(1,128)S(1)}, f32[1,2560]{1,0:T(1,128)}, u32[]{:S(2)}) copy-start(f32[1,2560]{1,0:T(1,128)} %conv_b.3) | copy-start | bytes 30724
  0.0 8.6 %copy-start.4 = (f32[1,2560]{1,0:T(1,128)S(1)}, f32[1,2560]{1,0:T(1,128)}, u32[]{:S(2)}) copy-start(f32[1,2560]{1,0:T(1,128)} %gain.3) | copy-start | bytes 30724
  0.0 8.6 %copy-start = (f32[1,16,2560]{2,1,0:T(8,128)S(1)}, f32[1,16,2560]{2,1,0:T(8,128)}, u32[]{:S(2)}) copy-start(f32[1,16,2560]{2,1,0:T(8,128)} %param.18) | copy-start | bytes 491524
  0.0 8.6 %copy-start.1 = (bf16[1,160,2560]{2,1,0:T(8,128)(2,1)S(1)}, bf16[1,160,2560]{2,1,0:T(8,128)(2,1)}, u32[]{:S(2)}) copy-start(bf16[1,160,2560]{2,1,0:T(8,128)(2,1)} %param.16) | copy-start | bytes 2457604
  0.0 8.6 %copy-start.3 = (bf16[1,4,2560]{2,1,0:T(4,128)(2,1)S(1)}, bf16[1,4,2560]{2,1,0:T(4,128)(2,1)}, u32[]{:S(2)}) copy-start(bf16[1,4,2560]{2,1,0:T(4,128)(2,1)} %param.13) | copy-start | bytes 61444
  1.0 7.6 %collective-permute-start = (bf16[8,2560]{1,0:T(8,128)(2,1)S(1)}, bf16[8,2560]{1,0:T(8,128)(2,1)S(1)}, u32[]{:S(2)}, u32[]{:S(2)}) collective-permute-start(bf16[8,2560]{1,0:T(8,128)(2,1)S(1)} %slice_bitcast_fusion), channel_id=1, source_target_pairs={{0,1},{1,2},{2,3},{3,4},{4,5},{5,6},{6,7},{8,9},{9,10},{10,11},{11... | collective-permute-start | bytes 122888 | tf_op jit(solution)/shard_map/ppermute | solution.py:42
  5.1 50.1 %collective-permute-start.2 = (bf16[1,8,2560]{2,1,0:T(8,128)(2,1)S(1)}, bf16[1,8,2560]{2,1,0:T(8,128)(2,1)S(1)}, u32[]{:S(2)}, u32[]{:S(2)}) collective-permute-start(bf16[1,8,2560]{2,1,0:T(8,128)(2,1)S(1)} %slice.21), channel_id=1, source_target_pairs={{0,1},{1,2},{2,3},{3,4},{4,5},{5,6},{6,7},{8,9},{9,10},{10,11},{11... | collective-permute-start | bytes 122888 | tf_op jit(solution)/shard_map/ppermute | solution.py:42
  51.4 7.1 %collective-permute-start.3 = (bf16[8,2560]{1,0:T(8,128)(2,1)S(1)}, bf16[8,2560]{1,0:T(8,128)(2,1)S(1)}, u32[]{:S(2)}, u32[]{:S(2)}) collective-permute-start(bf16[8,2560]{1,0:T(8,128)(2,1)S(1)} %slice.24), channel_id=1, source_target_pairs={{0,9},{1,10},{2,11},{3,12},{4,13},{5,14},{6,15},{7,16},{8,17},{9,1... | collective-permute-start | bytes 122888 | tf_op jit(solution)/shard_map/ppermute | solution.py:42
  53.3 12.2 %collective-permute-start.1 = (bf16[128,2560]{1,0:T(8,128)(2,1)S(1)}, bf16[128,2560]{1,0:T(8,128)(2,1)S(1)}, u32[]{:S(2)}, u32[]{:S(2)}) collective-permute-start(bf16[128,2560]{1,0:T(8,128)(2,1)S(1)} %carry_fix.2), channel_id=1, source_target_pairs={{0,8},{8,16},{16,24},{1,9},{9,17},{17,25},{2,10},{10,18},{18,26},{... | collective-permute-start | bytes 1966088 | tf_op jit(solution)/shard_map/ppermute | solution.py:42

commit v3 on v2

--- a/solution.py
+++ b/solution.py
@@ -80,16 +80,22 @@
                                             device_id={"seq": me + 2}, device_id_type=MESH)
 
     def to_even(j):
-        return pltpu.make_async_remote_copy(hout.at[j], hin.at[j], even_send.at[j], hin_recv.at[j],
-                                            device_id={"seq": me + 1}, device_id_type=MESH)
-
-    @pl.when(me > 0)
+        return pltpu.make_async_remote_copy(hin.at[j], hin.at[j], even_send.at[j], hin_recv.at[j],
+                                            device_id={"seq": me - 1}, device_id_type=MESH)
+
+    onward = jnp.logical_and(odd, earlier)
+
+    @pl.when(odd)
     def _():
         greet(me - 1)
 
-    @pl.when(jnp.logical_and(odd, earlier))
+    @pl.when(onward)
     def _():
         greet(me - 2)
+
+    @pl.when(jnp.logical_and(jnp.logical_not(odd), earlier))
+    def _():
+        greet(me + 1)
 
     @pl.when(jnp.logical_not(odd))
     def _():
@@ -98,9 +104,13 @@
         for j in range(chunks):
             to_pair(j).start()
 
-    @pl.when(later)
+    @pl.when(jnp.logical_and(later, onward))
     def _():
         pl.semaphore_wait(barrier, 2)
+
+    @pl.when(jnp.logical_and(odd, later != onward))
+    def _():
+        pl.semaphore_wait(barrier, 1)
 
     @pl.when(odd)
     def _():
@@ -125,6 +135,9 @@
         def _():
             hout[j] = decays[j] * hin[j] + pairs[j]
             to_odd(j).start()
+
+        @pl.when(onward)
+        def _():
             to_even(j).start()
 
     @pl.when(odd)
@@ -145,6 +158,10 @@
     def _():
         for j in range(chunks):
             to_odd(j).wait_send()
+
+    @pl.when(onward)
+    def _():
+        for j in range(chunks):
             to_even(j).wait_send()
 
 
@@ -327,7 +344,8 @@
     seq_zero = lax.axis_index("seq") == 0
     weights = (norm_gain, conv_weight[0], conv_bias, x_proj[0], dt_proj[0], dt_bias, a_rate[0], skip)
     current = acts[0]
-    prev_now, prev_feeds = passed_along((acts[0][-PAD:], feed[:, -PAD:, :]), "seq", 1)
+    tails = passed_along(jnp.concatenate([acts[:, -PAD:], feed[:, -PAD:]], 0), "seq", 1)
+    prev_now, prev_feeds = (tails[0], tails[1:])
     results = []
     for tick in range(TICKS):
         result = layer(current, prev_now, *weights)

time: 104 us -> 103 us (level)
  waiting for transfers between devices: 10.3 us -> 12.5 us
  starting transfers between devices: 9.14 us -> 7.24 us
  Pallas kernels: 78.4 us -> 76.8 us
    pallas_call x2, Pallas kernels: 32.7 us -> 30.3 us  [relay_carries(): pl.pallas_call(functools.partial(relay_kernel, size=size), out_shape=jax....]
    ppermute x4 -> x3, waiting for transfers between devices: 10.3 us -> 12.5 us  [passed_along(): lax.ppermute(value, axis, [(source, source + steps) for source in range(i...]
    ppermute x4 -> x3, starting transfers between devices: 9.14 us -> 7.24 us  [passed_along(): lax.ppermute(value, axis, [(source, source + steps) for source in range(i...]
  transfers between devices with their start and end apart: 4 -> 3, of which waited for: 2 -> 3; matrix products, arithmetic and copies ran while one was open for 2% -> 2% of each run, Pallas kernels for 41% -> 0%
where the time goes in v3:
time: 103 us; the launch traced here: 102 us
  Pallas kernels  76.8 us (75%)
  waiting for transfers between devices  12.5 us (12%)
  starting transfers between devices  7.24 us (7%)
  local copies, waits for them, and re-layouts  3.31 us (3%)
  other arithmetic  2.35 us (2%)
    pallas_call x2, Pallas kernels, relay_carries(): pl.pallas_call(functools.partial(relay_kernel, size=size), out_shape=jax....  30.3 us
    pallas_call x2, Pallas kernels, layer(): pl.pallas_call(scan_kernel, out_shape=(jax.ShapeDtypeStruct((rows, width)...  29.7 us
    pallas_call x2, Pallas kernels, layer(): pl.pallas_call(fix_kernel, out_shape=jax.ShapeDtypeStruct((rows, width),...  16.8 us
    ppermute x3, waiting for transfers between devices, passed_along(): lax.ppermute(value, axis, [(source, source + steps) for source in range(i...  12.5 us
    ppermute x3, starting transfers between devices, passed_along(): lax.ppermute(value, axis, [(source, source + steps) for source in range(i...  7.24 us
  transfers between devices with their start and end apart: 3, of which 3 were waited for; matrix products, arithmetic and copies ran while one was open for 2% of the time, Pallas kernels for 0%

profile of v3, /device:TPU:28, one launch (start us, length us, event | category | flops | bytes accessed | tf_op | source)
XLA Modules:
  0.0 102.4 jit_solution(7613373419587246551)
XLA Ops:
  0.0 0.8 slice.21
  0.8 0.0 copy-start
  0.8 0.0 copy-start.1
  0.8 0.0 copy-start.3
  0.8 0.0 copy-start.4
  0.8 0.0 copy-start.5
  0.8 0.0 copy-start.6
  0.8 0.0 copy-start.7
  0.9 0.9 slice.22
  1.8 3.4 %collective-permute-start = (bf16[2,8,2560]{2,1,0:T(8,128)(2,1)S(1)}, bf16[2,8,2560]{2,1,0:T(8,128)(2,1)S(1)}, u32[]{:S(2)}, u32[]{:S(2)}) collective-permute-start(bf16[2,8,2560]{2,1,0:T(8,128)(2,1)S(1)} %pad_maximum_fusion), channel_id=1, source_target_pairs={{0,1},{1,2},{2,3},{3,4},{4,5},{5,6},{6,7},{8,9},{9,10},{10,11},{11... | collective-permute-start | bytes 245768 | tf_op jit(solution)/shard_map/ppermute | solution.py:42
  5.2 1.5 %copy.11 = bf16[1,2560,192]{2,1,0:T(8,128)(2,1)S(1)} copy(bf16[1,2560,192]{1,2,0:T(8,128)(2,1)} %param.15) | data formatting | bytes 1966080 | tf_op args[5]
  6.7 2.3 %collective-permute-done = bf16[2,8,2560]{2,1,0:T(8,128)(2,1)S(1)} collective-permute-done((bf16[2,8,2560]{2,1,0:T(8,128)(2,1)S(1)}, bf16[2,8,2560]{2,1,0:T(8,128)(2,1)S(1)}, u32[]{:S(2)}, u32[]{:S(2)}) %collective-permute-start) | collective-permute-done | bytes 81952 | tf_op jit(solution)/shard_map/ppermute | solution.py:42
  9.0 0.0 copy-done
  9.0 0.0 copy-done.1
  9.0 0.0 copy-done.2
  9.0 0.0 copy-done.3
  9.0 0.0 copy-done.4
  9.0 0.0 copy-done.5
  9.1 0.0 copy-done.6
  9.1 0.0 copy-done.7
  9.1 14.9 %local_scan.2 = (f32[128,2560]{1,0:T(8,128)S(1)}, f32[16,2560]{1,0:T(8,128)S(1)}, f32[128,2560]{1,0:T(8,128)S(1)}, bf16[128,256]{1,0:T(8,128)(2,1)S(1)}) custom-call(bf16[128,2560]{1,0:T(8,128)(2,1)S(1)} %bitcast.31, bf16[8,2560]{1,0:T(8,128)(2,1)S(1)} %slice_bitcast_fusion.1.before, f32[1,2560]{1,0:T(1,128)S(1)} %copy-done.4, bf16[4,2560]{1,0:T(4,128)(2,1)S(1)} %bitcast.32, ...), custom_call_target="tpu_custom_call" | custom-call | tf_op jit(solution)/shard_map/local_scan/pallas_call | solution.py:309
  24.0 16.7 %carry_relay.2.incoming = f32[16,2560]{1,0:T(8,128)S(1)} custom-call(f32[16,2560]{1,0:T(8,128)S(1)} %get-tuple-element.16.ends, f32[1,2560]{1,0:T(1,128)S(1)} %slice.24.totals, f32[16,2560]{1,0:T(8,128)S(1)} %bitcast.22), custom_call_target="tpu_custom_call" | custom-call | tf_op jit(solution)/shard_map/carry_relay/pallas_call | solution.py:178
  40.7 8.4 %carry_fix.2 = bf16[128,2560]{1,0:T(8,128)(2,1)S(1)} custom-call(f32[128,2560]{1,0:T(8,128)S(1)} %get-tuple-element.13.local, f32[128,2560]{1,0:T(8,128)S(1)} %get-tuple-element.14.summed, bf16[128,256]{1,0:T(8,128)(2,1)S(1)} %get-tuple-element.15.cblk, f32[16,2560]{1,0:T(8,128)S(1)} %carry_relay.2.incoming, f32[16,2560]{1,0:T(8,128)S(1)} %bitcast.23), custom_call_target="tpu_custom_call" | custom-call | tf_op jit(solution)/shard_map/carry_fix/pallas_call | solution.py:331
  49.0 1.9 %collective-permute-start.2 = (bf16[8,2560]{1,0:T(8,128)(2,1)S(1)}, bf16[8,2560]{1,0:T(8,128)(2,1)S(1)}, u32[]{:S(2)}, u32[]{:S(2)}) collective-permute-start(bf16[8,2560]{1,0:T(8,128)(2,1)S(1)} %slice.30), channel_id=1, source_target_pairs={{0,9},{1,10},{2,11},{3,12},{4,13},{5,14},{6,15},{7,16},{8,17},{9,1... | collective-permute-start | bytes 122888 | tf_op jit(solution)/shard_map/ppermute | solution.py:42
  51.0 1.9 %collective-permute-start.1 = (bf16[128,2560]{1,0:T(8,128)(2,1)S(1)}, bf16[128,2560]{1,0:T(8,128)(2,1)S(1)}, u32[]{:S(2)}, u32[]{:S(2)}) collective-permute-start(bf16[128,2560]{1,0:T(8,128)(2,1)S(1)} %carry_fix.2), channel_id=1, source_target_pairs={{0,8},{8,16},{16,24},{1,9},{9,17},{17,25},{2,10},{10,18},{18,26},{... | collective-permute-start | bytes 1966088 | tf_op jit(solution)/shard_map/ppermute | solution.py:42
  52.9 3.3 %collective-permute-done.2 = bf16[8,2560]{1,0:T(8,128)(2,1)S(1)} collective-permute-done((bf16[8,2560]{1,0:T(8,128)(2,1)S(1)}, bf16[8,2560]{1,0:T(8,128)(2,1)S(1)}, u32[]{:S(2)}, u32[]{:S(2)}) %collective-permute-start.2) | collective-permute-done | bytes 40992 | tf_op jit(solution)/shard_map/ppermute | solution.py:42
  56.2 7.0 %collective-permute-done.1 = bf16[128,2560]{1,0:T(8,128)(2,1)S(1)} collective-permute-done((bf16[128,2560]{1,0:T(8,128)(2,1)S(1)}, bf16[128,2560]{1,0:T(8,128)(2,1)S(1)}, u32[]{:S(2)}, u32[]{:S(2)}) %collective-permute-start.1) | collective-permute-done | bytes 655392 | tf_op jit(solution)/shard_map/ppermute | solution.py:42
  63.2 1.2 %bitcast_select_fusion.cur = bf16[128,2560]{1,0:T(8,128)(2,1)S(1)} fusion(bf16[128,2560]{1,0:T(8,128)(2,1)S(1)} %collective-permute-done.1, bf16[1,128,2560]{2,1,0:T(8,128)(2,1)} %param.11, pred[]{:T(512)S(6)} %eq.6), kind=kLoop, calls=%fused_computation.1 | loop fusion | flops 327680 | bytes 1966081 | tf_op jit(solution)/shard_map/jit(_where)/select_n | solution.py:355
  64.3 14.9 %local_scan.3 = (f32[128,2560]{1,0:T(8,128)S(1)}, f32[16,2560]{1,0:T(8,128)S(1)}, f32[128,2560]{1,0:T(8,128)S(1)}, bf16[128,256]{1,0:T(8,128)(2,1)S(1)}) custom-call(bf16[128,2560]{1,0:T(8,128)(2,1)S(1)} %bitcast_select_fusion.cur, bf16[8,2560]{1,0:T(8,128)(2,1)S(1)} %fusion.before, f32[1,2560]{1,0:T(1,128)S(1)} %copy-done.4, bf16[4,2560]{1,0:T(4,128)(2,1)S(1)} %bitcast.33, ...), custom_call_target="tpu_custom_call" | custom-call | tf_op jit(solution)/shard_map/local_scan/pallas_call | solution.py:309
  79.2 13.6 %carry_relay.3.incoming = f32[16,2560]{1,0:T(8,128)S(1)} custom-call(f32[16,2560]{1,0:T(8,128)S(1)} %get-tuple-element.20.ends, f32[1,2560]{1,0:T(1,128)S(1)} %slice.27.totals, f32[16,2560]{1,0:T(8,128)S(1)} %bitcast.25), custom_call_target="tpu_custom_call" | custom-call | tf_op jit(solution)/shard_map/carry_relay/pallas_call | solution.py:178
  92.8 8.4 %carry_fix.3 = bf16[128,2560]{1,0:T(8,128)(2,1)S(1)} custom-call(f32[128,2560]{1,0:T(8,128)S(1)} %get-tuple-element.17.local, f32[128,2560]{1,0:T(8,128)S(1)} %get-tuple-element.18.summed, bf16[128,256]{1,0:T(8,128)(2,1)S(1)} %get-tuple-element.19.cblk, f32[16,2560]{1,0:T(8,128)S(1)} %carry_relay.3.incoming, f32[16,2560]{1,0:T(8,128)S(1)} %bitcast.26), custom_call_target="tpu_custom_call" | custom-call | tf_op jit(solution)/shard_map/carry_fix/pallas_call | solution.py:331
  101.2 1.2 %maximum_bitcast_fusion = bf16[2,1,128,2560]{3,2,1,0:T(8,128)(2,1)} fusion(bf16[1,128,2560]{2,1,0:T(8,128)(2,1)S(1)} %bitcast.30, bf16[1,128,2560]{2,1,0:T(8,128)(2,1)S(1)} %bitcast.29), kind=kLoop, calls=%fused_computation | loop fusion | flops 655360 | bytes 2621440 | tf_op jit(solution)/shard_map/broadcast_in_dim | solution.py:359
  (7 shorter events, 0.1 us)
Async XLA Ops:
  0.8 8.2 %copy-start = (f32[1,16,2560]{2,1,0:T(8,128)S(1)}, f32[1,16,2560]{2,1,0:T(8,128)}, u32[]{:S(2)}) copy-start(f32[1,16,2560]{2,1,0:T(8,128)} %param.18) | copy-start | bytes 491524
  0.8 8.2 %copy-start.1 = (bf16[1,160,2560]{2,1,0:T(8,128)(2,1)S(1)}, bf16[1,160,2560]{2,1,0:T(8,128)(2,1)}, u32[]{:S(2)}) copy-start(bf16[1,160,2560]{2,1,0:T(8,128)(2,1)} %param.16) | copy-start | bytes 2457604
  0.8 8.2 %copy-start.2 = (bf16[1,128,2560]{2,1,0:T(8,128)(2,1)S(1)}, bf16[1,128,2560]{2,1,0:T(8,128)(2,1)}, u32[]{:S(2)}) copy-start(bf16[1,128,2560]{2,1,0:T(8,128)(2,1)} %param.10) | copy-start | bytes 1966084
  0.8 8.2 %copy-start.3 = (bf16[1,4,2560]{2,1,0:T(4,128)(2,1)S(1)}, bf16[1,4,2560]{2,1,0:T(4,128)(2,1)}, u32[]{:S(2)}) copy-start(bf16[1,4,2560]{2,1,0:T(4,128)(2,1)} %param.13) | copy-start | bytes 61444
  0.8 8.2 %copy-start.4 = (f32[1,2560]{1,0:T(1,128)S(1)}, f32[1,2560]{1,0:T(1,128)}, u32[]{:S(2)}) copy-start(f32[1,2560]{1,0:T(1,128)} %gain.3) | copy-start | bytes 30724
  0.8 8.2 %copy-start.5 = (f32[1,2560]{1,0:T(1,128)S(1)}, f32[1,2560]{1,0:T(1,128)}, u32[]{:S(2)}) copy-start(f32[1,2560]{1,0:T(1,128)} %conv_b.3) | copy-start | bytes 30724
  0.8 8.2 %copy-start.6 = (f32[1,2560]{1,0:T(1,128)S(1)}, f32[1,2560]{1,0:T(1,128)}, u32[]{:S(2)}) copy-start(f32[1,2560]{1,0:T(1,128)} %dt_b.3) | copy-start | bytes 30724
  0.8 8.2 %copy-start.7 = (f32[1,2560]{1,0:T(1,128)S(1)}, f32[1,2560]{1,0:T(1,128)}, u32[]{:S(2)}) copy-start(f32[1,2560]{1,0:T(1,128)} %skip_w.3) | copy-start | bytes 30724
  1.8 7.2 %collective-permute-start = (bf16[2,8,2560]{2,1,0:T(8,128)(2,1)S(1)}, bf16[2,8,2560]{2,1,0:T(8,128)(2,1)S(1)}, u32[]{:S(2)}, u32[]{:S(2)}) collective-permute-start(bf16[2,8,2560]{2,1,0:T(8,128)(2,1)S(1)} %pad_maximum_fusion), channel_id=1, source_target_pairs={{0,1},{1,2},{2,3},{3,4},{4,5},{5,6},{6,7},{8,9},{9,10},{10,11},{11... | collective-permute-start | bytes 245768 | tf_op jit(solution)/shard_map/ppermute | solution.py:42
  49.0 7.1 %collective-permute-start.2 = (bf16[8,2560]{1,0:T(8,128)(2,1)S(1)}, bf16[8,2560]{1,0:T(8,128)(2,1)S(1)}, u32[]{:S(2)}, u32[]{:S(2)}) collective-permute-start(bf16[8,2560]{1,0:T(8,128)(2,1)S(1)} %slice.30), channel_id=1, source_target_pairs={{0,9},{1,10},{2,11},{3,12},{4,13},{5,14},{6,15},{7,16},{8,17},{9,1... | collective-permute-start | bytes 122888 | tf_op jit(solution)/shard_map/ppermute | solution.py:42
  51.0 12.2 %collective-permute-start.1 = (bf16[128,2560]{1,0:T(8,128)(2,1)S(1)}, bf16[128,2560]{1,0:T(8,128)(2,1)S(1)}, u32[]{:S(2)}, u32[]{:S(2)}) collective-permute-start(bf16[128,2560]{1,0:T(8,128)(2,1)S(1)} %carry_fix.2), channel_id=1, source_target_pairs={{0,8},{8,16},{16,24},{1,9},{9,17},{17,25},{2,10},{10,18},{18,26},{... | collective-permute-start | bytes 1966088 | tf_op jit(solution)/shard_map/ppermute | solution.py:42
